TPU v7x, 256 devices: a whole 4x4x8 slice. The times are simulated.
256 devices in a mesh: slab: 8 (over z), pencil: 32 (over y, x, core).
Axes of the slice: x: 4, y: 4, z: 8, core: 2. Of those that a mesh axis runs over, the one named last changes fastest.
Arguments:
- right_sides: float32 [8, 128, 128, 128], P(None, 'slab', 'pencil'), may hold values from -6 to 6
- spectrum: float32 [128, 128, 128], P('pencil', 'slab'), may hold values from 0.5 to 20, as said below
- noise_var: float32 [128, 128, 128], P('slab', 'pencil'), may hold values from 0.05 to 1
- observed: int32 [128, 128, 128], P('slab', 'pencil'), may hold values 0 or 1
Outputs:
- solution: float32 [8, 128, 128, 128], P(None, 'slab', 'pencil')
- noise_grad: float32 [128, 128, 128], P('slab', 'pencil')
Inputs may be any that keep to these rules, and one draw needn't show every extreme that they name: Even in every index: spectrum[a, b, c] equals spectrum[(-a) mod 128, (-b) mod 128, (-c) mod 128].
All inputs are finite; a program needn't handle non-finite values. No bound on the sum of `observed` on one device may be relied on, other than what follows from the above.
Results may differ from a plain program's by a relative error of at most 0.00021.
Values sent between devices are 32-bit elements; how exact they have to be, the bound alone decides.
A program may use at most 64 MiB of HBM per device.

v0:
```python
import functools
import math

import jax
import jax.numpy as jnp
from jax import lax
from jax.sharding import Mesh
from jax.sharding import PartitionSpec as P

NZ = 128
NY = 128
NX = 128
ITERS = 3
PENCIL = ("pencil_0", "pencil_1", "pencil_2")
SLAB_PENCIL = ("slab", "pencil_0", "pencil_1", "pencil_2")


precise = lax.Precision.HIGHEST


def over_axes(value, axes):
    return functools.reduce(lax.psum, axes, value)


def tables(length):
    points = jnp.arange(length, dtype=jnp.int32)
    phase_index = points[:, None] * points[None, :] % length
    angles = phase_index.astype(jnp.float32) * (2.0 * math.pi / length)
    return (jnp.cos(angles), jnp.sin(angles))


def full_table(length, forward):
    cosine, sine_table = tables(length)
    sign_factor = 1.0 if forward else -1.0
    real_row = jnp.stack((cosine, sign_factor * sine_table), axis=1)
    imag_row = jnp.stack((-sign_factor * sine_table, cosine), axis=1)
    return jnp.stack((real_row, imag_row))


def operate(field_block, eigen_block, seen_cells, noise_var):
    masked = field_block * seen_cells
    probe_count, z_local, y_local, extent = masked.shape
    pairs = masked.reshape(probe_count // 2, 2, z_local, y_local, extent)
    spec_x = jnp.einsum("qczyx,dkcx->dkyqz", pairs, full_table(extent, True), precision=precise)
    spec_x = spec_x.reshape(2, extent, y_local, probe_count // 2 * z_local)
    local_probes = spec_x.shape[3] // z_local
    pieces = lax.all_to_all(spec_x, PENCIL, split_axis=1, concat_axis=2, tiled=True)
    row_block = jnp.einsum(
        "ckyr,dmcy->dkmr", pieces, full_table(pieces.shape[2], True), precision=precise
    )
    row_block = row_block.reshape(row_block.shape[:3] + (local_probes, z_local))
    pieces = lax.all_to_all(row_block, "slab", split_axis=2, concat_axis=4, tiled=True)
    length = pieces.shape[4]
    spectral = jnp.einsum("ckjpz,dmcz->dkjpm", pieces, full_table(length, True), precision=precise)
    spectral = spectral * eigen_block[None, :, :, None, :]
    slab_block = jnp.einsum(
        "ckjpm,dzcm->dkjpz", spectral, full_table(length, False), precision=precise
    )
    pieces = lax.all_to_all(slab_block, "slab", split_axis=4, concat_axis=2, tiled=True)
    back_block = jnp.einsum(
        "ckmpz,dycm->dkypz", pieces, full_table(pieces.shape[2], False), precision=precise
    )
    back_block = back_block.reshape(back_block.shape[:3] + (local_probes * z_local,))
    pieces = lax.all_to_all(back_block, PENCIL, split_axis=2, concat_axis=1, tiled=True)
    length = pieces.shape[1]
    smooth = jnp.einsum("ckyr,dxck->rdyx", pieces, full_table(length, False), precision=precise)
    smooth = smooth.reshape(probe_count // 2, z_local, 2, y_local, extent)
    smooth = jnp.transpose(smooth, (0, 2, 1, 3, 4)).reshape(probe_count, z_local, y_local, extent)
    return seen_cells * smooth + noise_var * field_block


def symmetric(matrix):
    return 0.5 * (matrix + matrix.T)


def solve_spd(matrix, right_hand):
    factor = jnp.linalg.cholesky(symmetric(matrix))
    halfway = lax.linalg.triangular_solve(factor, right_hand, left_side=True, lower=True)
    return lax.linalg.triangular_solve(
        factor, halfway, left_side=True, lower=True, transpose_a=True
    )


def gram_local(left, right):
    column_count = left.shape[0]
    return jnp.dot(
        left.reshape(column_count, -1), right.reshape(column_count, -1).T, precision=precise
    )


def combine(field_block, coefficients):
    column_count = field_block.shape[0]
    mixed = jnp.dot(coefficients.T, field_block.reshape(column_count, -1), precision=precise)
    return mixed.reshape(field_block.shape)


def both_grams(residual, image_block):
    return (
        over_axes(gram_local(residual, residual), SLAB_PENCIL),
        over_axes(gram_local(residual, image_block), SLAB_PENCIL),
    )


def local(right_sides, spectrum, noise_var, observed):
    eigen_block = spectrum * (1.0 / (NX * NY * NZ))
    seen_cells = observed.astype(jnp.float32)
    solution = jnp.zeros_like(right_sides)
    residual = right_sides
    image_block = operate(residual, eigen_block, seen_cells, noise_var)
    gamma_now, delta_now = both_grams(residual, image_block)
    direction = residual
    along_image = image_block
    for iteration in range(ITERS):
        alpha_step = solve_spd(delta_now, gamma_now)
        solution = solution + combine(direction, alpha_step)
        if iteration + 1 < ITERS:
            residual = residual - combine(along_image, alpha_step)
            image_block = operate(residual, eigen_block, seen_cells, noise_var)
            gamma_next, product = both_grams(residual, image_block)
            beta_step = solve_spd(gamma_now, gamma_next)
            delta_now = product - jnp.dot(
                jnp.dot(beta_step.T, delta_now.T, precision=precise), beta_step, precision=precise
            )
            direction = residual + combine(direction, beta_step)
            along_image = image_block + combine(along_image, beta_step)
            gamma_now = gamma_next
    weights = right_sides[1:] * solution[1:]
    noise_grad = 0.5 * (solution[0] * solution[0] - jnp.mean(weights, axis=0))
    return (solution, noise_grad)


def solution(mesh):
    split = Mesh(
        mesh.devices.reshape(mesh.shape["slab"], 4, 4, 2),
        ("slab", "pencil_0", "pencil_1", "pencil_2"),
    )
    return jax.shard_map(
        local,
        mesh=split,
        in_specs=(
            P(None, "slab", PENCIL, None),
            P(PENCIL, "slab", None),
            P("slab", PENCIL, None),
            P("slab", PENCIL, None),
        ),
        out_specs=(P(None, "slab", PENCIL, None), P("slab", PENCIL, None)),
        check_vma=False,
    )
```

profile of v0, /device:TPU:1, one launch (start us, length us, event | category | flops | bytes accessed | tf_op | source)
XLA Modules:
  0.0 414.1 jit_solution(11745315092880318477)
XLA Ops:
  5.1 17.2 %all_to_all.216 = f32[32,1,2048]{2,1,0:T(1,128)S(1)} all-to-all(f32[32,1,2048]{2,1,0:T(1,128)S(1)} %reshape.316), channel_id=1, replica_groups=mesh['slab'=8,'pencil_0'=4,'pencil_1'=4,'pencil_2'=2] {'pencil_0','penci..., dimensions={0} | all-to-all | bytes 524288 | tf_op jit(solution)/shard_map/all_to_all | solution.py:47
  27.5 2.3 reshape.318
  29.8 8.4 %all-to-all-start.1 = ((f32[8,1,8192]{2,1,0:T(1,128)}), f32[8,1,8192]{2,1,0:T(1,128)S(1)}, u32[]{:S(2)}, u32[]{:S(2)}) async-start(f32[8,1,8192]{2,1,0:T(1,128)} %reshape.318), calls=%async_computation.1 | async-start | bytes 524288 | tf_op jit(solution)/shard_map/all_to_all | solution.py:52
  38.2 12.2 %all-to-all-done.1 = f32[8,1,8192]{2,1,0:T(1,128)S(1)} async-done(((f32[8,1,8192]{2,1,0:T(1,128)}), f32[8,1,8192]{2,1,0:T(1,128)S(1)}, u32[]{:S(2)}, u32[]{:S(2)}) %all-to-all-start.1) | async-done | bytes 262176 | tf_op jit(solution)/shard_map/all_to_all | solution.py:52
  53.2 2.6 copy.402
  61.9 14.1 %all_to_all.217 = f32[8,1,8192]{2,1,0:T(1,128)S(1)} all-to-all(f32[8,1,8192]{2,1,0:T(1,128)S(1)} %reshape.320), channel_id=1, replica_groups=mesh['slab'=8,'pencil_0'=4,'pencil_1'=4,'pencil_2'=2] {'slab'}, dimensions={0} | all-to-all | bytes 524288 | tf_op jit(solution)/shard_map/all_to_all | solution.py:59
  78.8 2.6 copy.405
  85.5 4.9 %all-to-all-start.3 = ((f32[32,1,2048]{2,1,0:T(1,128)}), f32[32,1,2048]{2,1,0:T(1,128)S(1)}, u32[]{:S(2)}, u32[]{:S(2)}) async-start(f32[32,1,2048]{2,1,0:T(1,128)} %reshape.322), calls=%async_computation.3 | async-start | bytes 524288 | tf_op jit(solution)/shard_map/all_to_all | solution.py:64
  91.1 8.3 %all-to-all-done.3 = f32[32,1,2048]{2,1,0:T(1,128)S(1)} async-done(((f32[32,1,2048]{2,1,0:T(1,128)}), f32[32,1,2048]{2,1,0:T(1,128)S(1)}, u32[]{:S(2)}, u32[]{:S(2)}) %all-to-all-start.3) | async-done | bytes 262176 | tf_op jit(solution)/shard_map/all_to_all | solution.py:64
  103.4 11.2 %all-reduce.2 = (f32[8,8]{1,0:T(8,128)S(1)}, f32[8,8]{1,0:T(8,128)S(1)}) all-reduce(f32[8,8]{1,0:T(8,128)S(1)} %convolution_bitcast_fusion.16, f32[8,8]{1,0:T(8,128)S(1)} %convolution_bitcast_fusion.17), channel_id=1, replica_groups=mesh['slab'=8,'pencil_0'=4,'pencil_1'=4,'pencil_2'=2] {'slab'}, use_global_device_ids=true, to_apply=%region_6.8 | all-reduce | flops 128 | bytes 1024 | tf_op jit(solution)/shard_map/psum | solution.py:22
  114.6 7.3 %all-reduce.8 = (f32[8,8]{1,0:T(8,128)S(1)}, f32[8,8]{1,0:T(8,128)S(1)}) all-reduce(f32[8,8]{1,0:T(8,128)S(1)} %get-tuple-element.17, f32[8,8]{1,0:T(8,128)S(1)} %get-tuple-element.18), channel_id=1, replica_groups=mesh['slab'=8,'pencil_0'=4,'pencil_1'=4,'pencil_2'=2] {'pencil_0'}, use_global_device_ids=true, to_apply=%region_7.9 | all-reduce | flops 128 | bytes 1024 | tf_op jit(solution)/shard_map/psum | solution.py:22
  121.9 7.3 %all-reduce.5 = (f32[8,8]{1,0:T(8,128)S(1)}, f32[8,8]{1,0:T(8,128)S(1)}) all-reduce(f32[8,8]{1,0:T(8,128)S(1)} %get-tuple-element.29, f32[8,8]{1,0:T(8,128)S(1)} %get-tuple-element.30), channel_id=1, replica_groups=mesh['slab'=8,'pencil_0'=4,'pencil_1'=4,'pencil_2'=2] {'pencil_1'}, use_global_device_ids=true, to_apply=%region_8.10 | all-reduce | flops 128 | bytes 1024 | tf_op jit(solution)/shard_map/psum | solution.py:22
  129.1 9.6 %all-reduce.11 = (f32[8,8]{1,0:T(8,128)S(1)}, f32[8,8]{1,0:T(8,128)S(1)}) all-reduce(f32[8,8]{1,0:T(8,128)S(1)} %get-tuple-element.23, f32[8,8]{1,0:T(8,128)S(1)} %get-tuple-element.24), channel_id=1, replica_groups=mesh['slab'=8,'pencil_0'=4,'pencil_1'=4,'pencil_2'=2] {'pencil_2'}, use_global_device_ids=true, to_apply=%region_9.11 | all-reduce | flops 128 | bytes 1024 | tf_op jit(solution)/shard_map/psum | solution.py:22
  143.9 12.0 %all_to_all.218 = f32[32,1,2048]{2,1,0:T(1,128)S(1)} all-to-all(f32[32,1,2048]{2,1,0:T(1,128)S(1)} %reshape.324), channel_id=1, replica_groups=mesh['slab'=8,'pencil_0'=4,'pencil_1'=4,'pencil_2'=2] {'pencil_0','penci..., dimensions={0} | all-to-all | bytes 524288 | tf_op jit(solution)/shard_map/all_to_all | solution.py:47
  159.7 2.4 copy.229
  162.1 2.3 reshape.326
  164.3 3.8 all-to-all-start.5
  168.2 12.1 %all-to-all-done.5 = f32[8,1,8192]{2,1,0:T(1,128)S(1)} async-done(((f32[8,1,8192]{2,1,0:T(1,128)}), f32[8,1,8192]{2,1,0:T(1,128)S(1)}, u32[]{:S(2)}, u32[]{:S(2)}) %all-to-all-start.5) | async-done | bytes 262176 | tf_op jit(solution)/shard_map/all_to_all | solution.py:52
  182.4 2.4 reshape.327
  184.8 2.6 copy.401
  191.1 2.4 copy.233
  193.5 2.3 reshape.328
  195.8 3.4 all-to-all-start.6
  200.7 10.2 %all-to-all-done.6 = f32[8,1,8192]{2,1,0:T(1,128)S(1)} async-done(((f32[8,1,8192]{2,1,0:T(1,128)}), f32[8,1,8192]{2,1,0:T(1,128)S(1)}, u32[]{:S(2)}, u32[]{:S(2)}) %all-to-all-start.6) | async-done | bytes 262176 | tf_op jit(solution)/shard_map/all_to_all | solution.py:59
  212.9 2.4 reshape.329
  215.3 2.6 copy.404
  221.9 4.8 %all-to-all-start.7 = ((f32[32,1,2048]{2,1,0:T(1,128)}), f32[32,1,2048]{2,1,0:T(1,128)S(1)}, u32[]{:S(2)}, u32[]{:S(2)}) async-start(f32[32,1,2048]{2,1,0:T(1,128)} %reshape.330), calls=%async_computation.7 | async-start | bytes 524288 | tf_op jit(solution)/shard_map/all_to_all | solution.py:64
  228.6 7.1 %all-to-all-done.7 = f32[32,1,2048]{2,1,0:T(1,128)S(1)} async-done(((f32[32,1,2048]{2,1,0:T(1,128)}), f32[32,1,2048]{2,1,0:T(1,128)S(1)}, u32[]{:S(2)}, u32[]{:S(2)}) %all-to-all-start.7) | async-done | bytes 262176 | tf_op jit(solution)/shard_map/all_to_all | solution.py:64
  239.7 11.2 %all-reduce.1 = (f32[8,8]{1,0:T(8,128)S(1)}, f32[8,8]{1,0:T(8,128)S(1)}) all-reduce(f32[8,8]{1,0:T(8,128)S(1)} %convolution_bitcast_fusion.14, f32[8,8]{1,0:T(8,128)S(1)} %convolution_bitcast_fusion.15), channel_id=1, replica_groups=mesh['slab'=8,'pencil_0'=4,'pencil_1'=4,'pencil_2'=2] {'slab'}, use_global_device_ids=true, to_apply=%region_14.0 | all-reduce | flops 128 | bytes 1024 | tf_op jit(solution)/shard_map/psum | solution.py:22
  250.9 7.3 %all-reduce.7 = (f32[8,8]{1,0:T(8,128)S(1)}, f32[8,8]{1,0:T(8,128)S(1)}) all-reduce(f32[8,8]{1,0:T(8,128)S(1)} %get-tuple-element.15, f32[8,8]{1,0:T(8,128)S(1)} %get-tuple-element.16), channel_id=1, replica_groups=mesh['slab'=8,'pencil_0'=4,'pencil_1'=4,'pencil_2'=2] {'pencil_0'}, use_global_device_ids=true, to_apply=%region_15.0 | all-reduce | flops 128 | bytes 1024 | tf_op jit(solution)/shard_map/psum | solution.py:22
  258.2 7.3 %all-reduce.4 = (f32[8,8]{1,0:T(8,128)S(1)}, f32[8,8]{1,0:T(8,128)S(1)}) all-reduce(f32[8,8]{1,0:T(8,128)S(1)} %get-tuple-element.27, f32[8,8]{1,0:T(8,128)S(1)} %get-tuple-element.28), channel_id=1, replica_groups=mesh['slab'=8,'pencil_0'=4,'pencil_1'=4,'pencil_2'=2] {'pencil_1'}, use_global_device_ids=true, to_apply=%region_16.0 | all-reduce | flops 128 | bytes 1024 | tf_op jit(solution)/shard_map/psum | solution.py:22
  265.5 9.6 %all-reduce.10 = (f32[8,8]{1,0:T(8,128)S(1)}, f32[8,8]{1,0:T(8,128)S(1)}) all-reduce(f32[8,8]{1,0:T(8,128)S(1)} %get-tuple-element.21, f32[8,8]{1,0:T(8,128)S(1)} %get-tuple-element.22), channel_id=1, replica_groups=mesh['slab'=8,'pencil_0'=4,'pencil_1'=4,'pencil_2'=2] {'pencil_2'}, use_global_device_ids=true, to_apply=%region_17.0 | all-reduce | flops 128 | bytes 1024 | tf_op jit(solution)/shard_map/psum | solution.py:22
  281.9 3.9 all-to-all-start.8
  287.0 7.7 %all-to-all-done.8 = f32[32,1,2048]{2,1,0:T(1,128)S(1)} async-done(((f32[32,1,2048]{2,1,0:T(1,128)}), f32[32,1,2048]{2,1,0:T(1,128)S(1)}, u32[]{:S(2)}, u32[]{:S(2)}) %all-to-all-start.8) | async-done | bytes 262176 | tf_op jit(solution)/shard_map/all_to_all | solution.py:47
  299.4 2.3 reshape.334
  301.7 3.6 all-to-all-start.9
  306.8 10.7 %all-to-all-done.9 = f32[8,1,8192]{2,1,0:T(1,128)S(1)} async-done(((f32[8,1,8192]{2,1,0:T(1,128)}), f32[8,1,8192]{2,1,0:T(1,128)S(1)}, u32[]{:S(2)}, u32[]{:S(2)}) %all-to-all-start.9) | async-done | bytes 262176 | tf_op jit(solution)/shard_map/all_to_all | solution.py:52
  320.3 2.6 copy.400
  327.4 2.3 reshape.336
  329.7 3.7 all-to-all-start.10
  334.4 10.6 %all-to-all-done.10 = f32[8,1,8192]{2,1,0:T(1,128)S(1)} async-done(((f32[8,1,8192]{2,1,0:T(1,128)}), f32[8,1,8192]{2,1,0:T(1,128)S(1)}, u32[]{:S(2)}, u32[]{:S(2)}) %all-to-all-start.10) | async-done | bytes 262176 | tf_op jit(solution)/shard_map/all_to_all | solution.py:59
  347.8 2.6 copy.403
  354.4 4.6 %all-to-all-start.11 = ((f32[32,1,2048]{2,1,0:T(1,128)}), f32[32,1,2048]{2,1,0:T(1,128)S(1)}, u32[]{:S(2)}, u32[]{:S(2)}) async-start(f32[32,1,2048]{2,1,0:T(1,128)} %reshape.338), calls=%async_computation.11 | async-start | bytes 524288 | tf_op jit(solution)/shard_map/all_to_all | solution.py:64
  360.7 7.3 %all-to-all-done.11 = f32[32,1,2048]{2,1,0:T(1,128)S(1)} async-done(((f32[32,1,2048]{2,1,0:T(1,128)}), f32[32,1,2048]{2,1,0:T(1,128)S(1)}, u32[]{:S(2)}, u32[]{:S(2)}) %all-to-all-start.11) | async-done | bytes 262176 | tf_op jit(solution)/shard_map/all_to_all | solution.py:64
  372.0 11.2 %all-reduce = (f32[8,8]{1,0:T(8,128)S(1)}, f32[8,8]{1,0:T(8,128)S(1)}) all-reduce(f32[8,8]{1,0:T(8,128)S(1)} %convolution_bitcast_fusion.12, f32[8,8]{1,0:T(8,128)S(1)} %convolution_bitcast_fusion.13), channel_id=1, replica_groups=mesh['slab'=8,'pencil_0'=4,'pencil_1'=4,'pencil_2'=2] {'slab'}, use_global_device_ids=true, to_apply=%region_22.0 | all-reduce | flops 128 | bytes 1024 | tf_op jit(solution)/shard_map/psum | solution.py:22
  383.2 7.3 %all-reduce.6 = (f32[8,8]{1,0:T(8,128)S(1)}, f32[8,8]{1,0:T(8,128)S(1)}) all-reduce(f32[8,8]{1,0:T(8,128)S(1)} %get-tuple-element.13, f32[8,8]{1,0:T(8,128)S(1)} %get-tuple-element.14), channel_id=1, replica_groups=mesh['slab'=8,'pencil_0'=4,'pencil_1'=4,'pencil_2'=2] {'pencil_0'}, use_global_device_ids=true, to_apply=%region_23.0 | all-reduce | flops 128 | bytes 1024 | tf_op jit(solution)/shard_map/psum | solution.py:22
  390.5 7.3 %all-reduce.3 = (f32[8,8]{1,0:T(8,128)S(1)}, f32[8,8]{1,0:T(8,128)S(1)}) all-reduce(f32[8,8]{1,0:T(8,128)S(1)} %get-tuple-element.25, f32[8,8]{1,0:T(8,128)S(1)} %get-tuple-element.26), channel_id=1, replica_groups=mesh['slab'=8,'pencil_0'=4,'pencil_1'=4,'pencil_2'=2] {'pencil_1'}, use_global_device_ids=true, to_apply=%region_24.0 | all-reduce | flops 128 | bytes 1024 | tf_op jit(solution)/shard_map/psum | solution.py:22
  397.8 9.6 %all-reduce.9 = (f32[8,8]{1,0:T(8,128)S(1)}, f32[8,8]{1,0:T(8,128)S(1)}) all-reduce(f32[8,8]{1,0:T(8,128)S(1)} %get-tuple-element.19, f32[8,8]{1,0:T(8,128)S(1)} %get-tuple-element.20), channel_id=1, replica_groups=mesh['slab'=8,'pencil_0'=4,'pencil_1'=4,'pencil_2'=2] {'pencil_2'}, use_global_device_ids=true, to_apply=%region_25.29 | all-reduce | flops 128 | bytes 1024 | tf_op jit(solution)/shard_map/psum | solution.py:22
  (180 shorter events, 99.0 us)
Async XLA Ops:
  26.0 12.2 %copy-start.6 = (f32[4,16,128]{2,1,0:T(8,128)S(1)}, f32[4,16,128]{2,1,0:T(8,128)}, u32[]{:S(2)}) copy-start(f32[4,16,128]{2,1,0:T(8,128)} %param.10) | copy-start | bytes 98308
  29.8 20.6 %all-to-all-start.1 = ((f32[8,1,8192]{2,1,0:T(1,128)}), f32[8,1,8192]{2,1,0:T(1,128)S(1)}, u32[]{:S(2)}, u32[]{:S(2)}) async-start(f32[8,1,8192]{2,1,0:T(1,128)} %reshape.318), calls=%async_computation.1 | async-start | bytes 524288 | tf_op jit(solution)/shard_map/all_to_all | solution.py:52
  81.4 9.0 %copy-start = (f32[8,16,4,128]{3,2,1,0:T(4,128)S(1)}, f32[8,16,4,128]{3,2,1,0:T(4,128)}, u32[]{:S(2)}) copy-start(f32[8,16,4,128]{3,2,1,0:T(4,128)} %param.9) | copy-start | bytes 786436
  85.5 13.9 %all-to-all-start.3 = ((f32[32,1,2048]{2,1,0:T(1,128)}), f32[32,1,2048]{2,1,0:T(1,128)S(1)}, u32[]{:S(2)}, u32[]{:S(2)}) async-start(f32[32,1,2048]{2,1,0:T(1,128)} %reshape.322), calls=%async_computation.3 | async-start | bytes 524288 | tf_op jit(solution)/shard_map/all_to_all | solution.py:64
  100.6 2.1 copy-start.5
  164.3 16.0 %all-to-all-start.5 = ((f32[8,1,8192]{2,1,0:T(1,128)}), f32[8,1,8192]{2,1,0:T(1,128)S(1)}, u32[]{:S(2)}, u32[]{:S(2)}) async-start(f32[8,1,8192]{2,1,0:T(1,128)} %reshape.326), calls=%async_computation.5 | async-start | bytes 524288 | tf_op jit(solution)/shard_map/all_to_all | solution.py:52
  195.8 15.1 %all-to-all-start.6 = ((f32[8,1,8192]{2,1,0:T(1,128)}), f32[8,1,8192]{2,1,0:T(1,128)S(1)}, u32[]{:S(2)}, u32[]{:S(2)}) async-start(f32[8,1,8192]{2,1,0:T(1,128)} %reshape.328), calls=%async_computation.6 | async-start | bytes 524288 | tf_op jit(solution)/shard_map/all_to_all | solution.py:59
  221.9 13.8 %all-to-all-start.7 = ((f32[32,1,2048]{2,1,0:T(1,128)}), f32[32,1,2048]{2,1,0:T(1,128)S(1)}, u32[]{:S(2)}, u32[]{:S(2)}) async-start(f32[32,1,2048]{2,1,0:T(1,128)} %reshape.330), calls=%async_computation.7 | async-start | bytes 524288 | tf_op jit(solution)/shard_map/all_to_all | solution.py:64
  281.9 12.9 %all-to-all-start.8 = ((f32[32,1,2048]{2,1,0:T(1,128)}), f32[32,1,2048]{2,1,0:T(1,128)S(1)}, u32[]{:S(2)}, u32[]{:S(2)}) async-start(f32[32,1,2048]{2,1,0:T(1,128)} %reshape.332), calls=%async_computation.8 | async-start | bytes 524288 | tf_op jit(solution)/shard_map/all_to_all | solution.py:47
  285.9 12.0 %copy-start.1 = (f32[8,8192]{1,0:T(8,128)}, f32[8,8192]{1,0:T(8,128)S(1)}, u32[]{:S(2)}) copy-start(f32[8,8192]{1,0:T(8,128)S(1)} %reshape.206) | copy-start | bytes 786436
  301.7 15.8 %all-to-all-start.9 = ((f32[8,1,8192]{2,1,0:T(1,128)}), f32[8,1,8192]{2,1,0:T(1,128)S(1)}, u32[]{:S(2)}, u32[]{:S(2)}) async-start(f32[8,1,8192]{2,1,0:T(1,128)} %reshape.334), calls=%async_computation.9 | async-start | bytes 524288 | tf_op jit(solution)/shard_map/all_to_all | solution.py:52
  325.9 8.1 %copy-start.2 = (f32[8,8192]{1,0:T(8,128)S(1)}, f32[8,8192]{1,0:T(8,128)}, u32[]{:S(2)}) copy-start(f32[8,8192]{1,0:T(8,128)} %copy-done.1) | copy-start | bytes 786436
  329.7 15.3 %all-to-all-start.10 = ((f32[8,1,8192]{2,1,0:T(1,128)}), f32[8,1,8192]{2,1,0:T(1,128)S(1)}, u32[]{:S(2)}, u32[]{:S(2)}) async-start(f32[8,1,8192]{2,1,0:T(1,128)} %reshape.336), calls=%async_computation.10 | async-start | bytes 524288 | tf_op jit(solution)/shard_map/all_to_all | solution.py:59
  352.5 7.8 %copy-start.4 = (f32[8,16,4,128]{3,0,2,1:T(8,128)S(1)}, f32[8,16,4,128]{3,0,2,1:T(8,128)}, u32[]{:S(2)}) copy-start(f32[8,16,4,128]{3,0,2,1:T(8,128)} %fusion.113) | copy-start | bytes 786436
  354.4 13.6 %all-to-all-start.11 = ((f32[32,1,2048]{2,1,0:T(1,128)}), f32[32,1,2048]{2,1,0:T(1,128)S(1)}, u32[]{:S(2)}, u32[]{:S(2)}) async-start(f32[32,1,2048]{2,1,0:T(1,128)} %reshape.338), calls=%async_computation.11 | async-start | bytes 524288 | tf_op jit(solution)/shard_map/all_to_all | solution.py:64
  371.1 41.8 %copy-start.3 = (f32[8,16,4,128]{3,0,2,1:T(8,128)S(1)}, f32[8,16,4,128]{3,0,2,1:T(8,128)}, u32[]{:S(2)}) copy-start(f32[8,16,4,128]{3,0,2,1:T(8,128)} %get-tuple-element.37) | copy-start | bytes 786436
where the time goes:
time: 421 us; the launch traced here: 414 us
  blocking collectives  149 us (35%)
  waiting for transfers between devices  86.2 us (20%)
  local copies, waits for them, and re-layouts  78 us (19%)
  starting transfers between devices  41 us (10%)
  other arithmetic  33.9 us (8%)
  matrix products  23.5 us (6%)
    psum x12, blocking collectives, over_axes(): return functools.reduce(lax.psum, axes, value)  106 us
    all_to_all x3, waiting for transfers between devices, operate(): lax.all_to_all(row_block, 'slab', split_axis=2, concat_axis=4, tiled=True)  35 us
    unnamed x39, local copies, waits for them, and re-layouts  32.3 us
    all_to_all x2, blocking collectives, operate(): lax.all_to_all(spec_x, PENCIL, split_axis=1, concat_axis=2, tiled=True)  29.2 us
    all_to_all x3, waiting for transfers between devices, operate(): lax.all_to_all(back_block, PENCIL, split_axis=2, concat_axis=1, tiled=True)  22.7 us
    all_to_all x2, waiting for transfers between devices, operate(): lax.all_to_all(slab_block, 'slab', split_axis=4, concat_axis=2, tiled=True)  20.8 us
    all_to_all x3, starting transfers between devices, operate(): lax.all_to_all(row_block, 'slab', split_axis=2, concat_axis=4, tiled=True)  15.8 us
    all_to_all x3, starting transfers between devices, operate(): lax.all_to_all(back_block, PENCIL, split_axis=2, concat_axis=1, tiled=True)  14.3 us
  transfers between devices with their start and end apart: 9, of which 9 were waited for; matrix products, arithmetic and copies ran while one was open for 2% of the time, Pallas kernels for 0%

commit v1 on v0

v1 whole, which is shorter than its diff:
```python
import functools

import jax
import jax.numpy as jnp
import ml_dtypes
import numpy as np
from jax import lax
from jax.experimental import pallas as pl
from jax.experimental.pallas import tpu as pltpu
from jax.sharding import PartitionSpec as P

MESH = pl.DeviceIdType.MESH
F32 = jnp.float32
BF16 = jnp.bfloat16
N = 128
SLAB, PENCIL = 8, 32
INV = 1.0 / (N * N * N)


def split_np(a):
    hi = a.astype(ml_dtypes.bfloat16)
    lo = (a - hi.astype(np.float64)).astype(ml_dtypes.bfloat16)
    return hi, lo


def tables():
    k = np.arange(N)
    ang = 2.0 * np.pi * (np.outer(k, k) % N) / N
    c, s = np.cos(ang), np.sin(ang)
    wx = np.concatenate([c, s], 1)
    place = np.arange(PENCIL * 8)
    a_in, a_out = (-place) % 8, place % 8
    y_in, part_in = 4 * (place // 8) + a_in % 4, a_in // 4
    y_out, part_out = 4 * (place // 8) + a_out % 4, a_out // 4
    wy_f = np.zeros((256, 256))
    wy_i = np.zeros((256, 256))
    for part in range(2):
        for i in range(256):
            wy_f[part * N:(part + 1) * N, i] = (c if part == part_in[i] else (s if part == 0 else -s))[:, y_in[i]]
            wy_i[i, part * N:(part + 1) * N] = (c if part == part_out[i] else (-s if part == 1 else s))[:, y_out[i]]
    wz_f = np.block([[c, -s], [s, c]])
    wz_i = np.block([[c, s], [-s, c]])
    stack = lambda w: np.concatenate(split_np(w), 0)
    return [stack(w) for w in (wx, wy_f, wz_f, wz_i, wy_i)]


def split(v):
    hi = v.astype(BF16)
    return hi, (v - hi.astype(F32)).astype(BF16)


def dot(a, b):
    return lax.dot_general(a, b, (((1,), (0,)), ((), ())), preferred_element_type=F32)


def left_mul(w, v):
    m = w.shape[0] // 2
    hi, lo = split(v)
    t = dot(w[...], hi)
    return t[:m] + (t[m:] + dot(w[:m], lo))


def right_mul(v, w):
    m, k = v.shape
    hi, lo = split(v)
    t = dot(jnp.concatenate([hi, lo], 0), w[:k])
    return t[:m] + (t[m:] + dot(hi, w[k:]))


def iota(shape, axis):
    return lax.broadcasted_iota(jnp.int32, shape, axis)


def chunk_swap(v):
    rows = v.shape[0]
    chunk = iota((rows // 8, 8, 128), 2) // 16
    v = pltpu.roll(v, 0, 1, stride=16, stride_axis=0).reshape(rows // 8, 8, 128)
    for bit in (1, 2, 4):
        v = jnp.where((chunk & bit) != 0, pltpu.roll(v, 8 - bit, 1), v)
    return pltpu.roll(v.reshape(rows, 128), 0, 1, stride=16, stride_axis=0)


def matmul8(a, b):
    out = a[:, 0:1] * b[0:1, :]
    for k in range(1, 8):
        out = out + a[:, k:k + 1] * b[k:k + 1, :]
    return out


def columns_of_transpose(a):
    eye = iota((8, 128), 0) == iota((8, 128), 1)
    return [jnp.sum(jnp.where(eye, a[k:k + 1, :], 0.0), axis=1, keepdims=True) for k in range(8)]


def transpose8(a):
    lane = iota((8, 128), 1)
    out = jnp.zeros((8, 128), F32)
    for k, col in enumerate(columns_of_transpose(a)):
        out = jnp.where(lane == k, col, out)
    return out


def matmul8_tn(a, b):
    cols = columns_of_transpose(a)
    out = cols[0] * b[0:1, :]
    for k in range(1, 8):
        out = out + cols[k] * b[k:k + 1, :]
    return out


def sym8(a):
    return 0.5 * (a + transpose8(a))


def solve8(matrix, rhs):
    row = iota((8, 128), 0)
    aug = jnp.where(iota((8, 128), 1) < 8, sym8(matrix), pltpu.roll(rhs, 8, 1))
    for k in range(8):
        pivot_row = aug[k:k + 1, :] / aug[k:k + 1, k:k + 1]
        aug = jnp.where(row == k, pivot_row, aug - aug[:, k:k + 1] * pivot_row)
    return jnp.where(iota((8, 128), 1) < 8, pltpu.roll(aug, 120, 1), 0.0)


def kernel(rs_ref, spec_ref, noise_ref, seen_ref, wx, wyf, wzf, wzi, wyi, sol_ref, ng_ref,
           r0, u0, w1, w2, r1, ar1, d1, ad1, r2, e, xs, seen, noise, lam, coef,
           sendf, recvf, sendb, recvb, ar_own, ar_plane, ar_mid, ar_slab,
           fs_sem, fr_sem, bs_sem, br_sem, lam_sems, arp_s, arp_r, ars_s, ars_r, enter):
    s = lax.axis_index("slab")
    p = lax.axis_index("pencil")

    barrier = pltpu.get_barrier_semaphore()

    @pl.loop(1, PENCIL)
    def _(o):
        pl.semaphore_signal(barrier, inc=1, device_id=(s, p ^ o), device_id_type=MESH)

    @pl.loop(1, SLAB)
    def _(o):
        pl.semaphore_signal(barrier, inc=1, device_id=((s + o) & 7, p), device_id_type=MESH)

    lane = iota((128, 128), 1)
    sign = jnp.where(lane < 64, 1.0, -1.0).astype(F32)

    for q in range(4):
        rows = [rs_ref[pl.ds((2 * q + c) * 64 + y, 16, stride=4), :] for c in range(2) for y in range(4)]
        r0[q] = jnp.concatenate(rows, 0).T
    rows = [noise_ref[pl.ds(y, 16, stride=4), :] for y in range(4)]
    noise[...] = jnp.concatenate(rows + rows, 0).T
    rows = [seen_ref[pl.ds(y, 16, stride=4), :].astype(F32) for y in range(4)]
    seen[...] = jnp.concatenate(rows + rows, 0).T

    def x_forward(k, h, v):
        mask = seen[...]
        m = jnp.concatenate([v[2 * h] * mask, v[2 * h + 1] * mask], 1)
        sg = jnp.concatenate([sign, sign], 1)
        turned = jnp.concatenate([pltpu.roll(m[:, :128], 64, 1), pltpu.roll(m[:, 128:], 64, 1)], 1) * sg
        out = left_mul(wx, jnp.concatenate([m, turned], 0))
        sendf[k, h, 0:128, :] = out[:, :128]
        sendf[k, h, 128:256, :] = out[:, 128:]

    def x_inverse(k, h, v, out_ref):
        a, b = recvb[k, h, 0:128, :], recvb[k, h, 128:256, :]
        m = jnp.concatenate([a, b], 1)
        sg = jnp.concatenate([sign, sign], 1)
        turned = jnp.concatenate([pltpu.roll(a, 64, 1), pltpu.roll(b, 64, 1)], 1) * (-sg)
        out = left_mul(wx, jnp.concatenate([m, turned], 0))
        for b in range(2):
            out_ref[2 * h + b] = seen[...] * out[:, b * 128:(b + 1) * 128] + noise[...] * v[2 * h + b]

    def middle(k, h):
        t = chunk_swap(recvf[k, h])
        t = left_mul(wyf, t)
        t = right_mul(jnp.concatenate([t[:128], t[128:]], 1), wzf)
        scale = lam[...] * INV
        t = t * jnp.concatenate([scale, scale], 1)
        t = right_mul(t, wzi)
        t = left_mul(wyi, jnp.concatenate([t[:, :128], t[:, 128:]], 0))
        sendb[k, h] = chunk_swap(t)

    def everyone(f):
        for offsets in ((4,), (3, 5), (2, 6), (1, 7), (0,)):
            first = 1 if offsets[0] == 0 else 0

            @pl.loop(first, PENCIL)
            def _(o):
                for so in offsets:
                    f((s + so) & 7, p ^ o)

    plane_row = lambda ts, tp: (ts & 1) * 128 + 4 * tp + (ts >> 1)
    seat_row = lambda ts, tp: tp * 8 + ts
    back_row = lambda ts, tp: tp * 8 + ((8 - ts) & 7)

    def exchange(src, dst, src_row, dst_row, ssem, rsem):
        here = dst_row(s, p)

        def one(ts, tp):
            pltpu.make_async_remote_copy(
                src_ref=src.at[pl.ds(src_row(ts, tp), 1), :], dst_ref=dst.at[pl.ds(here, 1), :],
                send_sem=ssem, recv_sem=rsem, device_id=(ts, tp), device_id_type=MESH).start()
        everyone(one)
        dst[pl.ds(here, 1), :] = src[pl.ds(src_row(s, p), 1), :]

    def wait_rows(ref, n, sem):
        pltpu.make_async_copy(ref.at[pl.ds(0, n), :], ref.at[pl.ds(0, n), :], sem).wait()

    def forward_send(k, h):
        exchange(sendf.at[k, h], recvf.at[k, h], plane_row, seat_row, fs_sem.at[k, h], fr_sem.at[k, h])

    def backward_send(k, h):
        exchange(sendb.at[k, h], recvb.at[k, h], back_row, plane_row, bs_sem.at[k, h], br_sem.at[k, h])

    def gram(u, v, at):
        def step(i, acc):
            rows = pl.ds(pl.multiple_of(i * 8, 8), 8)
            us = [u[q, rows, :] for q in range(4)]
            vs = [v[q, rows, :] for q in range(4)]
            turned = [pltpu.roll(t, 64, 1) for t in vs]
            return tuple(acc[q * 8 + t * 4 + r] + us[q] * (turned if t else vs)[r]
                         for q in range(4) for t in range(2) for r in range(4))
        acc = lax.fori_loop(0, 16, step, tuple(jnp.zeros((8, 128), F32) for _ in range(32)))
        r8, l8 = iota((8, 128), 0), iota((8, 128), 1)
        total = jnp.zeros((1, 128), F32)
        for q in range(4):
            tile = jnp.concatenate([jnp.sum(acc[q * 8 + t], axis=0, keepdims=True) for t in range(8)], 0)
            for c in range(2):
                sums = jnp.sum(jnp.where((l8 // 64) == c, tile, 0.0), axis=1, keepdims=True)
                column = 2 * (r8 & 3) + (c ^ (r8 >> 2))
                hit = l8 == (at - (2 * q + c) * 8) % 128 + column
                total = total + jnp.sum(jnp.where(hit, sums, 0.0), axis=0, keepdims=True)
        return total

    def plane_start(g, row):
        ar_own[g, 0:1, :] = row
        ar_plane[g, pl.ds(p, 1), :] = row

        @pl.loop(1, PENCIL)
        def _(o):
            pltpu.make_async_remote_copy(
                src_ref=ar_own.at[g, pl.ds(0, 1), :], dst_ref=ar_plane.at[g, pl.ds(p, 1), :],
                send_sem=arp_s.at[g], recv_sem=arp_r.at[g], device_id=(s, p ^ o), device_id_type=MESH).start()

    def slab_start(g):
        wait_rows(ar_plane.at[g], PENCIL - 1, arp_r.at[g])
        row = jnp.sum(ar_plane[g], axis=0, keepdims=True)
        ar_mid[g, 0:1, :] = row
        ar_slab[g, pl.ds(s, 1), :] = row
        for o in (4, 3, 5, 2, 6, 1, 7):
            pltpu.make_async_remote_copy(
                src_ref=ar_mid.at[g, pl.ds(0, 1), :], dst_ref=ar_slab.at[g, pl.ds(s, 1), :],
                send_sem=ars_s.at[g], recv_sem=ars_r.at[g], device_id=((s + o) & 7, p), device_id_type=MESH).start()

    def gram_finish(g):
        wait_rows(ar_slab.at[g], SLAB - 1, ars_r.at[g])
        row = jnp.sum(ar_slab[g], axis=0, keepdims=True)
        both = pltpu.roll(jnp.broadcast_to(row, (8, 128)), 0, 1, stride=8, stride_axis=0)
        clean = iota((8, 128), 1) < 8
        return jnp.where(clean, both, 0.0), jnp.where(clean, pltpu.roll(both, 64, 1), 0.0)

    def mix(out, base, terms):
        for slot, (v, small) in enumerate(terms):
            for r in range(4):
                wide = jnp.where(iota((8, 128), 1) < 64, small[:, 2 * r:2 * r + 1], small[:, 2 * r + 1:2 * r + 2])
                low = iota((1, 128), 1) < 64
                for q in range(4):
                    even, odd = wide[2 * q:2 * q + 1, :], wide[2 * q + 1:2 * q + 2, :]
                    coef[slot, r, 2 * q:2 * q + 1, :] = jnp.where(low, even, odd)
                    coef[slot, r, 2 * q + 1:2 * q + 2, :] = jnp.where(low, odd, even)

        @pl.loop(0, 16)
        def _(i):
            rows = pl.ds(pl.multiple_of(i * 8, 8), 8)
            outs = [base[r, rows, :] if base is not None else None for r in range(4)]
            for slot, (v, _small) in enumerate(terms):
                for q in range(4):
                    t = v[q, rows, :]
                    turned = pltpu.roll(t, 64, 1)
                    for r in range(4):
                        add = t * coef[slot, r, 2 * q:2 * q + 1, :] + turned * coef[slot, r, 2 * q + 1:2 * q + 2, :]
                        outs[r] = add if outs[r] is None else outs[r] + add
            for r in range(4):
                out[r, rows, :] = outs[r]

    x_forward(0, 0, r0)
    x_forward(0, 1, r0)

    pl.semaphore_wait(barrier, PENCIL - 1 + SLAB - 1)

    @pl.loop(1, SLAB)
    def _(o):
        pl.semaphore_signal(enter, inc=1, device_id=((s + o) & 7, p), device_id_type=MESH)
    pl.semaphore_wait(enter, SLAB - 1)

    def lam_rows(owner):
        return lam.at[pl.ds(pl.multiple_of(16 * owner, 16), 16), :]

    for o in (4, 3, 5, 2, 6, 1, 7):
        ts = (s + o) & 7
        pltpu.make_async_remote_copy(
            src_ref=spec_ref.at[ts >> 1], dst_ref=lam_rows(s), send_sem=lam_sems.at[0], recv_sem=lam_sems.at[1],
            device_id=(ts, p), device_id_type=MESH).start()
    lam[pl.ds(pl.multiple_of(16 * s, 16), 16), :] = spec_ref[s >> 1]

    forward_send(0, 0)
    forward_send(0, 1)

    def halves(f):
        @pl.loop(0, 2)
        def _(h):
            f(h)

    def middles(k, between=None):
        def one(h):
            wait_rows(recvf.at[k, h], 255, fr_sem.at[k, h])
            middle(k, h)
            backward_send(k, h)
            if between is not None:
                pl.when(h == 0)(between)
        halves(one)

    def inverses(k, v, out, onward):
        def one(h):
            wait_rows(recvb.at[k, h], 255, br_sem.at[k, h])
            x_inverse(k, h, v, out)
            if onward:
                x_forward(k + 1, h, out)
                forward_send(k + 1, h)
        halves(one)

    g00 = gram(r0, r0, 0)
    wait_rows(lam, 112, lam_sems.at[1])
    middles(0)
    inverses(0, r0, u0, True)
    plane_start(0, g00 + gram(r0, u0, 64))
    middles(1, lambda: slab_start(0))
    gamma0, delta0 = gram_finish(0)
    alpha0 = solve8(delta0, gamma0)
    mix(r1, r0, [(u0, -alpha0)])
    mix(xs, None, [(r0, alpha0)])
    g11 = gram(r1, r1, 0)
    inverses(1, u0, w1, True)
    mix(ar1, u0, [(w1, -alpha0)])
    plane_start(1, g11 + gram(r1, ar1, 64))
    middles(2, lambda: slab_start(1))
    gamma1, product1 = gram_finish(1)
    beta0 = solve8(gamma0, gamma1)
    delta1 = product1 - matmul8_tn(beta0, matmul8(delta0, beta0))
    alpha1 = solve8(delta1, gamma1)
    mix(d1, r1, [(r0, beta0)])
    mix(ad1, ar1, [(u0, beta0)])
    mix(r2, r1, [(ad1, -alpha1)])
    mix(e, ar1, [(w1, -(alpha1 + matmul8(beta0, alpha1)))])
    mix(xs, xs, [(d1, alpha1)])
    plane_start(2, gram(r2, r2, 0) + gram(r2, e, 64))
    alpha01 = matmul8(alpha0, alpha1)
    slab_start(2)
    inverses(2, w1, w2, False)
    plane_start(3, gram(r2, w2, 0))
    gamma2, part2 = gram_finish(2)
    beta1 = solve8(gamma1, gamma2)
    older = matmul8_tn(beta1, matmul8(delta1, beta1))
    mix(d1, r2, [(d1, beta1)])
    slab_start(3)
    rest2, _ = gram_finish(3)
    delta2 = sym8(part2 + matmul8(rest2, alpha01)) - older
    alpha2 = solve8(delta2, gamma2)
    mix(xs, xs, [(d1, alpha2)])

    acc = jnp.zeros((128, 128), F32)
    for q in range(4):
        sol = xs[q]
        acc = acc + jnp.where((lane < 64) & (q == 0), 0.0, r0[q] * sol)
        back = sol.T
        for c in range(2):
            for y in range(4):
                sol_ref[pl.ds((2 * q + c) * 64 + y, 16, stride=4), :] = back[c * 64 + y * 16:c * 64 + y * 16 + 16, :]
    mean = (acc + pltpu.roll(acc, 64, 1)) * (1.0 / 7.0)
    back = (0.5 * (xs[0] * xs[0] - mean)).T
    for y in range(4):
        ng_ref[pl.ds(y, 16, stride=4), :] = back[y * 16:y * 16 + 16, :]

    for k in range(3):
        for h in range(2):
            wait_rows(sendf.at[k, h], 255, fs_sem.at[k, h])
            wait_rows(sendb.at[k, h], 255, bs_sem.at[k, h])
    wait_rows(lam, 112, lam_sems.at[0])
    for g in range(4):
        wait_rows(ar_plane.at[g], PENCIL - 1, arp_s.at[g])
        wait_rows(ar_slab.at[g], SLAB - 1, ars_s.at[g])


def local(right_sides, spectrum, noise_var, observed):
    ws = [jnp.asarray(w) for w in tables()]
    block = lambda: pltpu.VMEM((4, 128, 128), F32)
    square = lambda: pltpu.VMEM((128, 128), F32)
    rows = lambda *shape: pltpu.VMEM(shape, F32)
    dma = pltpu.SemaphoreType.DMA
    sol, ng = pl.pallas_call(
        kernel,
        out_shape=(jax.ShapeDtypeStruct((512, 128), F32), jax.ShapeDtypeStruct((64, 128), F32)),
        in_specs=[pl.BlockSpec(memory_space=pltpu.VMEM)] * 9,
        out_specs=[pl.BlockSpec(memory_space=pltpu.VMEM)] * 2,
        scratch_shapes=[block() for _ in range(11)] + [square() for _ in range(3)] + [rows(1, 4, 8, 128)]
        + [rows(3, 2, 256, 128) for _ in range(4)]
        + [rows(4, 8, 128), rows(4, 32, 128), rows(4, 8, 128), rows(4, 8, 128)]
        + [dma((3, 2)) for _ in range(4)] + [dma((2,))] + [dma((4,)) for _ in range(4)]
        + [pltpu.SemaphoreType.REGULAR],
        compiler_params=pltpu.CompilerParams(collective_id=0, has_side_effects=True),
        name="block_cg",
    )(right_sides.reshape(512, 128), spectrum, noise_var.reshape(64, 128), observed.reshape(64, 128), *ws)
    return sol.reshape(8, 16, 4, 128), ng.reshape(16, 4, 128)


def solution(mesh):
    return jax.shard_map(
        local,
        mesh=mesh,
        in_specs=(
            P(None, "slab", "pencil", None),
            P("pencil", "slab", None),
            P("slab", "pencil", None),
            P("slab", "pencil", None),
        ),
        out_specs=(P(None, "slab", "pencil", None), P("slab", "pencil", None)),
        check_vma=False,
    )
```

time: 421 us -> 107 us (0.25); the launches traced: 414 us -> 106 us
  blocking collectives: 149 us -> 0 us
  Pallas kernels: 0 us -> 103 us
  waiting for transfers between devices: 86.2 us -> 0 us
  local copies, waits for them, and re-layouts: 78 us -> 2.3 us
  starting transfers between devices: 41 us -> 0 us
  other arithmetic: 33.9 us -> 0 us
  matrix products: 23.5 us -> 0 us
    psum x12 -> x0, blocking collectives: 106 us -> none  [over_axes(): return functools.reduce(lax.psum, axes, value)]
    pallas_call x0 -> x1, Pallas kernels: none -> 103 us  [local(): pl.pallas_call(kernel, out_shape=(jax.ShapeDtypeStruct((512, 128), F32),...]
    all_to_all x9 -> x0, waiting for transfers between devices: 86.2 us -> none  [the longest x3 35 us: operate(): lax.all_to_all(row_block, 'slab', split_axis=2, concat_axis=4, tiled=True)]
    all_to_all x3 -> x0, blocking collectives: 43.3 us -> none  [the longest x2 29.2 us: operate(): lax.all_to_all(spec_x, PENCIL, split_axis=1, concat_axis=2, tiled=True)]
    all_to_all x9 -> x0, starting transfers between devices: 41 us -> none  [the longest x3 15.8 us: operate(): lax.all_to_all(row_block, 'slab', split_axis=2, concat_axis=4, tiled=True)]
    all_to_all x25 -> x0, local copies, waits for them, and re-layouts: 31.6 us -> none  [the longest x6 14.3 us: operate(): lax.all_to_all(slab_block, 'slab', split_axis=4, concat_axis=2, tiled=True)]
    unnamed x39 -> x4, local copies, waits for them, and re-layouts: 32.3 us -> 2.3 us
    dot_general x36 -> x0, matrix products: 21.6 us -> none  [the longest x8 4.21 us: combine(): jnp.dot(coefficients.T, field_block.reshape(column_count, -1), precision=...]
  transfers between devices with their start and end apart: 9 -> 0, of which waited for: 9 -> 0; matrix products, arithmetic and copies ran while one was open for 2% -> 0% of each run, Pallas kernels for 0% -> 0%
where the time goes in v1:
time: 107 us; the launch traced here: 106 us
  Pallas kernels  103 us (96%)
  local copies, waits for them, and re-layouts  2.3 us (2%)
    pallas_call x1, Pallas kernels, local(): pl.pallas_call(kernel, out_shape=(jax.ShapeDtypeStruct((512, 128), F32),...  103 us
    unnamed x4, local copies, waits for them, and re-layouts  2.3 us

profile of v1, /device:TPU:1, one launch (start us, length us, event | category | flops | bytes accessed | tf_op | source)
XLA Modules:
  0.0 106.4 jit_solution(12201006368277761680)
XLA Ops:
  0.6 103.5 %block_cg.1 = (f32[512,128]{1,0:T(8,128)}, f32[64,128]{1,0:T(8,128)}) custom-call(f32[512,128]{1,0:T(8,128)} %bitcast.6, f32[4,16,128]{2,1,0:T(8,128)} %spec_ref.1, f32[64,128]{1,0:T(8,128)} %bitcast.7, s32[64,128]{1,0:T(8,128)} %bitcast.8, bf16[256,256]{1,0:T(8,128)(2,1)} %constant.10.clone.wx, bf16[512,256]{1,0:T(8,128)(2,1)} %constant.11.clone.wyf, ...), custom_call_target="tpu_custom_call" | custom-call | tf_op jit(solution)/shard_map/block_cg/pallas_call | solution.py:397
  104.1 0.0 copy-start
  104.1 1.7 %copy.13 = f32[8,16,4,128]{3,2,1,0:T(4,128)} copy(f32[8,16,4,128]{3,2,1,0:T(4,128)} %bitcast.5) | data formatting | bytes 524288
  105.8 0.0 copy-done
  105.8 0.6 copy.14
Async XLA Ops:
  104.1 1.7 %copy-start = (f32[64,128]{1,0:T(8,128)S(1)}, f32[64,128]{1,0:T(8,128)}, u32[]{:S(2)}) copy-start(f32[64,128]{1,0:T(8,128)} %get-tuple-element.5) | copy-start | bytes 98308

commit v2 on v1

--- a/solution.py
+++ b/solution.py
@@ -27,7 +27,9 @@
     k = np.arange(N)
     ang = 2.0 * np.pi * (np.outer(k, k) % N) / N
     c, s = np.cos(ang), np.sin(ang)
-    wx = np.concatenate([c, s], 1)
+    kx = 4 * (k % 32) + k // 32
+    wx_f = np.concatenate([c[kx], s[kx]], 1)
+    wx_i = np.concatenate([c[:, kx], s[:, kx]], 1)
     place = np.arange(PENCIL * 8)
     a_in, a_out = (-place) % 8, place % 8
     y_in, part_in = 4 * (place // 8) + a_in % 4, a_in // 4
@@ -41,7 +43,15 @@
     wz_f = np.block([[c, -s], [s, c]])
     wz_i = np.block([[c, s], [-s, c]])
     stack = lambda w: np.concatenate(split_np(w), 0)
-    return [stack(w) for w in (wx, wy_f, wz_f, wz_i, wy_i)]
+    lane_sum = np.zeros((2, N, N), ml_dtypes.bfloat16)
+    place_of = np.zeros((2, 32, N), np.float32)
+    for g in range(2):
+        for i in range(8):
+            for j in range(8):
+                lane = (64 * g - 8 * i) % N + j
+                lane_sum[g, (i & 1) * 64:(i & 1) * 64 + 64, lane] = 1
+                place_of[g, (i >> 1) * 8 + ((i ^ j) & 1) * 4 + (j >> 1), lane] = 1
+    return [stack(w) for w in (wx_f, wy_f, wz_f, wz_i, wy_i, wx_i)] + [lane_sum, place_of]
 
 
 def split(v):
@@ -100,14 +110,6 @@
     return out
 
 
-def matmul8_tn(a, b):
-    cols = columns_of_transpose(a)
-    out = cols[0] * b[0:1, :]
-    for k in range(1, 8):
-        out = out + cols[k] * b[k:k + 1, :]
-    return out
-
-
 def sym8(a):
     return 0.5 * (a + transpose8(a))
 
@@ -121,10 +123,13 @@
     return jnp.where(iota((8, 128), 1) < 8, pltpu.roll(aug, 120, 1), 0.0)
 
 
-def kernel(rs_ref, spec_ref, noise_ref, seen_ref, wx, wyf, wzf, wzi, wyi, sol_ref, ng_ref,
-           r0, u0, w1, w2, r1, ar1, d1, ad1, r2, e, xs, seen, noise, lam, coef,
-           sendf, recvf, sendb, recvb, ar_own, ar_plane, ar_mid, ar_slab,
-           fs_sem, fr_sem, bs_sem, br_sem, lam_sems, arp_s, arp_r, ars_s, ars_r, enter):
+def kernel(*refs):
+    given, (sol_ref, ng_ref), held = refs[:12], refs[12:14], refs[14:26]
+    (r0, u0, w1, w2, r1, ar1, d1, r2, e, xs, seen, noise, lam, coef,
+     sendf, recvf, sendb, recvb, ar_own, ar_plane, ar_mid, ar_slab, ar_all,
+     in_sem, fs_sem, fr_sem, bs_sem, br_sem, lam_sems, arp_s, arp_r, ars_s, ars_r, all_sems, enter) = refs[26:]
+    rs_ref, seen_ref, wxf, noise_ref, spec_ref, wyf, wzf, wzi, wyi, wxi, lane_sum, place = held
+    loads = [pltpu.make_async_copy(given[i], held[i], in_sem.at[i]) for i in range(12)]
     s = lax.axis_index("slab")
     p = lax.axis_index("pencil")
 
@@ -138,9 +143,14 @@
     def _(o):
         pl.semaphore_signal(barrier, inc=1, device_id=((s + o) & 7, p), device_id_type=MESH)
 
+    for load in loads:
+        load.start()
+
     lane = iota((128, 128), 1)
     sign = jnp.where(lane < 64, 1.0, -1.0).astype(F32)
 
+    for load in loads[:4]:
+        load.wait()
     for q in range(4):
         rows = [rs_ref[pl.ds((2 * q + c) * 64 + y, 16, stride=4), :] for c in range(2) for y in range(4)]
         r0[q] = jnp.concatenate(rows, 0).T
@@ -154,16 +164,17 @@
         m = jnp.concatenate([v[2 * h] * mask, v[2 * h + 1] * mask], 1)
         sg = jnp.concatenate([sign, sign], 1)
         turned = jnp.concatenate([pltpu.roll(m[:, :128], 64, 1), pltpu.roll(m[:, 128:], 64, 1)], 1) * sg
-        out = left_mul(wx, jnp.concatenate([m, turned], 0))
-        sendf[k, h, 0:128, :] = out[:, :128]
-        sendf[k, h, 128:256, :] = out[:, 128:]
+        out = left_mul(wxf, jnp.concatenate([m, turned], 0))
+        for l in range(4):
+            for b in range(2):
+                sendf[k, h, (2 * l + b) * 32:(2 * l + b) * 32 + 32, :] = out[32 * l:32 * l + 32, b * 128:b * 128 + 128]
 
     def x_inverse(k, h, v, out_ref):
-        a, b = recvb[k, h, 0:128, :], recvb[k, h, 128:256, :]
+        a, b = (jnp.concatenate([recvb[k, h, (2 * l + b) * 32:(2 * l + b) * 32 + 32, :] for l in range(4)], 0) for b in range(2))
         m = jnp.concatenate([a, b], 1)
         sg = jnp.concatenate([sign, sign], 1)
         turned = jnp.concatenate([pltpu.roll(a, 64, 1), pltpu.roll(b, 64, 1)], 1) * (-sg)
-        out = left_mul(wx, jnp.concatenate([m, turned], 0))
+        out = left_mul(wxi, jnp.concatenate([m, turned], 0))
         for b in range(2):
             out_ref[2 * h + b] = seen[...] * out[:, b * 128:(b + 1) * 128] + noise[...] * v[2 * h + b]
 
@@ -177,57 +188,73 @@
         t = left_mul(wyi, jnp.concatenate([t[:, :128], t[:, 128:]], 0))
         sendb[k, h] = chunk_swap(t)
 
-    def everyone(f):
-        for offsets in ((4,), (3, 5), (2, 6), (1, 7), (0,)):
-            first = 1 if offsets[0] == 0 else 0
-
-            @pl.loop(first, PENCIL)
+    def everyone(src, dst, base, chip_step, core_step, ssem, rsem):
+        seat, core = p >> 1, p & 1
+
+        def to(chip, c, row):
+            pltpu.make_async_remote_copy(
+                src_ref=src.at[pl.ds(row, 1), :], dst_ref=dst, send_sem=ssem, recv_sem=rsem,
+                device_id=(chip << 1) | c, device_id_type=pl.DeviceIdType.LOGICAL).start()
+
+        def to_chip(chip, row):
+            for c in range(2):
+                to(chip, c, row + core_step * c)
+
+        for offsets in ((4,), (3, 5), (2, 6), (1, 7)):
+            slabs = [(s + so) & 7 for so in offsets]
+            pre = [(ts * 16, base(ts)) for ts in slabs]
+
+            @pl.loop(0, 8)
             def _(o):
-                for so in offsets:
-                    f((s + so) & 7, p ^ o)
-
-    plane_row = lambda ts, tp: (ts & 1) * 128 + 4 * tp + (ts >> 1)
-    seat_row = lambda ts, tp: tp * 8 + ts
-    back_row = lambda ts, tp: tp * 8 + ((8 - ts) & 7)
-
-    def exchange(src, dst, src_row, dst_row, ssem, rsem):
-        here = dst_row(s, p)
-
-        def one(ts, tp):
-            pltpu.make_async_remote_copy(
-                src_ref=src.at[pl.ds(src_row(ts, tp), 1), :], dst_ref=dst.at[pl.ds(here, 1), :],
-                send_sem=ssem, recv_sem=rsem, device_id=(ts, tp), device_id_type=MESH).start()
-        everyone(one)
-        dst[pl.ds(here, 1), :] = src[pl.ds(src_row(s, p), 1), :]
+                for u in range(2):
+                    there = seat ^ (2 * o + u)
+                    step = chip_step * there
+                    for first, row in pre:
+                        to_chip(first + there, row + step)
+
+        @pl.loop(1, 16)
+        def _(o):
+            there = seat ^ o
+            to_chip(s * 16 + there, base(s) + chip_step * there)
+        to(s * 16 + seat, 1 - core, base(s) + chip_step * seat + core_step * (1 - core))
 
     def wait_rows(ref, n, sem):
         pltpu.make_async_copy(ref.at[pl.ds(0, n), :], ref.at[pl.ds(0, n), :], sem).wait()
 
+    me = s * 32 + p
+
     def forward_send(k, h):
-        exchange(sendf.at[k, h], recvf.at[k, h], plane_row, seat_row, fs_sem.at[k, h], fr_sem.at[k, h])
+        seat_row = p * 8 + s
+        everyone(sendf.at[k, h], recvf.at[k, h, pl.ds(seat_row, 1), :], lambda ts: 32 * ts, 2, 1,
+                 fs_sem.at[k, h], fr_sem.at[k, h])
+        recvf[k, h, pl.ds(seat_row, 1), :] = sendf[k, h, pl.ds(me, 1), :]
 
     def backward_send(k, h):
-        exchange(sendb.at[k, h], recvb.at[k, h], back_row, plane_row, bs_sem.at[k, h], br_sem.at[k, h])
+        everyone(sendb.at[k, h], recvb.at[k, h, pl.ds(me, 1), :], lambda ts: (8 - ts) & 7, 16, 8,
+                 bs_sem.at[k, h], br_sem.at[k, h])
+        recvb[k, h, pl.ds(me, 1), :] = sendb[k, h, pl.ds(p * 8 + ((8 - s) & 7), 1), :]
 
     def gram(u, v, at):
-        def step(i, acc):
-            rows = pl.ds(pl.multiple_of(i * 8, 8), 8)
-            us = [u[q, rows, :] for q in range(4)]
-            vs = [v[q, rows, :] for q in range(4)]
-            turned = [pltpu.roll(t, 64, 1) for t in vs]
-            return tuple(acc[q * 8 + t * 4 + r] + us[q] * (turned if t else vs)[r]
-                         for q in range(4) for t in range(2) for r in range(4))
-        acc = lax.fori_loop(0, 16, step, tuple(jnp.zeros((8, 128), F32) for _ in range(32)))
-        r8, l8 = iota((8, 128), 0), iota((8, 128), 1)
-        total = jnp.zeros((1, 128), F32)
-        for q in range(4):
-            tile = jnp.concatenate([jnp.sum(acc[q * 8 + t], axis=0, keepdims=True) for t in range(8)], 0)
-            for c in range(2):
-                sums = jnp.sum(jnp.where((l8 // 64) == c, tile, 0.0), axis=1, keepdims=True)
-                column = 2 * (r8 & 3) + (c ^ (r8 >> 2))
-                hit = l8 == (at - (2 * q + c) * 8) % 128 + column
-                total = total + jnp.sum(jnp.where(hit, sums, 0.0), axis=0, keepdims=True)
-        return total
+        acc = [None] * 32
+        for i in range(16):
+            us = [u[q, 8 * i:8 * i + 8, :] for q in range(4)]
+            vs = [v[q, 8 * i:8 * i + 8, :] for q in range(4)]
+            vs = vs + [pltpu.roll(t, 64, 1) for t in vs]
+            for q in range(4):
+                for t in range(8):
+                    term = us[q] * vs[t]
+                    acc[q * 8 + t] = term if i == 0 else acc[q * 8 + t] + term
+        tiles = jnp.concatenate(acc, 0)
+        hi = tiles.astype(BF16)
+        rest = tiles - hi.astype(F32)
+        mid = rest.astype(BF16)
+        low = (rest - mid.astype(F32)).astype(BF16)
+        sums = dot(jnp.concatenate([hi, mid, low], 0), lane_sum[at // 64])
+        sums = sums[:256] + (sums[256:512] + sums[512:])
+        parts = [sums[8 * t:8 * t + 8] * place[at // 64, t:t + 1, :] for t in range(32)]
+        while len(parts) > 1:
+            parts = [x + y for x, y in zip(parts[0::2], parts[1::2])]
+        return jnp.sum(parts[0], axis=0, keepdims=True)
 
     def plane_start(g, row):
         ar_own[g, 0:1, :] = row
@@ -251,10 +278,24 @@
 
     def gram_finish(g):
         wait_rows(ar_slab.at[g], SLAB - 1, ars_r.at[g])
-        row = jnp.sum(ar_slab[g], axis=0, keepdims=True)
+        return unfold(jnp.sum(ar_slab[g], axis=0, keepdims=True))
+
+    def all_start(row):
+        ar_own[2, 0:1, :] = row
+        ar_all[pl.ds(me, 1), :] = row
+        everyone(ar_own.at[2], ar_all.at[pl.ds(me, 1), :], lambda ts: 0, 0, 0, all_sems.at[0], all_sems.at[1])
+
+    def unfold(row):
         both = pltpu.roll(jnp.broadcast_to(row, (8, 128)), 0, 1, stride=8, stride_axis=0)
         clean = iota((8, 128), 1) < 8
         return jnp.where(clean, both, 0.0), jnp.where(clean, pltpu.roll(both, 64, 1), 0.0)
+
+    def all_finish():
+        wait_rows(ar_all, 255, all_sems.at[1])
+        tiles = [ar_all[8 * i:8 * i + 8, :] for i in range(32)]
+        while len(tiles) > 1:
+            tiles = [x + y for x, y in zip(tiles[0::2], tiles[1::2])]
+        return unfold(jnp.sum(tiles[0], axis=0, keepdims=True))
 
     def mix(out, base, terms):
         for slot, (v, small) in enumerate(terms):
@@ -266,9 +307,8 @@
                     coef[slot, r, 2 * q:2 * q + 1, :] = jnp.where(low, even, odd)
                     coef[slot, r, 2 * q + 1:2 * q + 2, :] = jnp.where(low, odd, even)
 
-        @pl.loop(0, 16)
-        def _(i):
-            rows = pl.ds(pl.multiple_of(i * 8, 8), 8)
+        for i in range(16):
+            rows = slice(8 * i, 8 * i + 8)
             outs = [base[r, rows, :] if base is not None else None for r in range(4)]
             for slot, (v, _small) in enumerate(terms):
                 for q in range(4):
@@ -282,6 +322,9 @@
 
     x_forward(0, 0, r0)
     x_forward(0, 1, r0)
+    for load in loads[4:]:
+        load.wait()
+    g00 = gram(r0, r0, 0)
 
     pl.semaphore_wait(barrier, PENCIL - 1 + SLAB - 1)
 
@@ -326,44 +369,42 @@
                 forward_send(k + 1, h)
         halves(one)
 
-    g00 = gram(r0, r0, 0)
     wait_rows(lam, 112, lam_sems.at[1])
     middles(0)
     inverses(0, r0, u0, True)
     plane_start(0, g00 + gram(r0, u0, 64))
+    eye = jnp.where(iota((8, 128), 0) == iota((8, 128), 1), 1.0, 0.0)
     middles(1, lambda: slab_start(0))
     gamma0, delta0 = gram_finish(0)
     alpha0 = solve8(delta0, gamma0)
     mix(r1, r0, [(u0, -alpha0)])
-    mix(xs, None, [(r0, alpha0)])
     g11 = gram(r1, r1, 0)
     inverses(1, u0, w1, True)
     mix(ar1, u0, [(w1, -alpha0)])
     plane_start(1, g11 + gram(r1, ar1, 64))
+    inverse0 = solve8(gamma0, eye)
+    older0 = matmul8(inverse0, matmul8(delta0, inverse0))
     middles(2, lambda: slab_start(1))
     gamma1, product1 = gram_finish(1)
-    beta0 = solve8(gamma0, gamma1)
-    delta1 = product1 - matmul8_tn(beta0, matmul8(delta0, beta0))
+    beta0 = matmul8(inverse0, gamma1)
+    delta1 = product1 - matmul8(gamma1, matmul8(older0, gamma1))
     alpha1 = solve8(delta1, gamma1)
+    beta_alpha = matmul8(beta0, alpha1)
+    alpha01 = matmul8(alpha0, alpha1)
+    mix(r2, r1, [(ar1, -alpha1), (u0, -beta_alpha)])
+    mix(e, ar1, [(w1, -(alpha1 + beta_alpha))])
+    g22 = gram(r2, r2, 0)
+    inverses(2, w1, w2, False)
+    mix(e, e, [(w2, alpha01)])
+    all_start(g22 + gram(r2, e, 64))
     mix(d1, r1, [(r0, beta0)])
-    mix(ad1, ar1, [(u0, beta0)])
-    mix(r2, r1, [(ad1, -alpha1)])
-    mix(e, ar1, [(w1, -(alpha1 + matmul8(beta0, alpha1)))])
-    mix(xs, xs, [(d1, alpha1)])
-    plane_start(2, gram(r2, r2, 0) + gram(r2, e, 64))
-    alpha01 = matmul8(alpha0, alpha1)
-    slab_start(2)
-    inverses(2, w1, w2, False)
-    plane_start(3, gram(r2, w2, 0))
-    gamma2, part2 = gram_finish(2)
-    beta1 = solve8(gamma1, gamma2)
-    older = matmul8_tn(beta1, matmul8(delta1, beta1))
-    mix(d1, r2, [(d1, beta1)])
-    slab_start(3)
-    rest2, _ = gram_finish(3)
-    delta2 = sym8(part2 + matmul8(rest2, alpha01)) - older
+    mix(xs, None, [(r0, alpha0), (d1, alpha1)])
+    inverse1 = solve8(gamma1, eye)
+    older1 = matmul8(inverse1, matmul8(delta1, inverse1))
+    gamma2, product2 = all_finish()
+    delta2 = product2 - matmul8(gamma2, matmul8(older1, gamma2))
     alpha2 = solve8(delta2, gamma2)
-    mix(xs, xs, [(d1, alpha2)])
+    mix(xs, xs, [(r2, alpha2), (d1, matmul8(matmul8(inverse1, gamma2), alpha2))])
 
     acc = jnp.zeros((128, 128), F32)
     for q in range(4):
@@ -383,7 +424,8 @@
             wait_rows(sendf.at[k, h], 255, fs_sem.at[k, h])
             wait_rows(sendb.at[k, h], 255, bs_sem.at[k, h])
     wait_rows(lam, 112, lam_sems.at[0])
-    for g in range(4):
+    wait_rows(ar_all, 255, all_sems.at[0])
+    for g in range(2):
         wait_rows(ar_plane.at[g], PENCIL - 1, arp_s.at[g])
         wait_rows(ar_slab.at[g], SLAB - 1, ars_s.at[g])
 
@@ -394,19 +436,21 @@
     square = lambda: pltpu.VMEM((128, 128), F32)
     rows = lambda *shape: pltpu.VMEM(shape, F32)
     dma = pltpu.SemaphoreType.DMA
+    operands = [right_sides.reshape(512, 128), observed.reshape(64, 128), ws[0], noise_var.reshape(64, 128), spectrum] + ws[1:]
     sol, ng = pl.pallas_call(
         kernel,
-        out_shape=(jax.ShapeDtypeStruct((512, 128), F32), jax.ShapeDtypeStruct((64, 128), F32)),
-        in_specs=[pl.BlockSpec(memory_space=pltpu.VMEM)] * 9,
+        out_shape=(pltpu.VMEM((512, 128), F32), pltpu.VMEM((64, 128), F32)),
+        in_specs=[pl.BlockSpec(memory_space=pl.ANY)] * 12,
         out_specs=[pl.BlockSpec(memory_space=pltpu.VMEM)] * 2,
-        scratch_shapes=[block() for _ in range(11)] + [square() for _ in range(3)] + [rows(1, 4, 8, 128)]
+        scratch_shapes=[pltpu.VMEM(a.shape, a.dtype) for a in operands]
+        + [block() for _ in range(10)] + [square() for _ in range(3)] + [rows(2, 4, 8, 128)]
         + [rows(3, 2, 256, 128) for _ in range(4)]
-        + [rows(4, 8, 128), rows(4, 32, 128), rows(4, 8, 128), rows(4, 8, 128)]
-        + [dma((3, 2)) for _ in range(4)] + [dma((2,))] + [dma((4,)) for _ in range(4)]
+        + [rows(3, 8, 128), rows(2, 32, 128), rows(2, 8, 128), rows(2, 8, 128), rows(256, 128)]
+        + [dma((12,))] + [dma((3, 2)) for _ in range(4)] + [dma((2,))] + [dma((2,)) for _ in range(4)] + [dma((2,))]
         + [pltpu.SemaphoreType.REGULAR],
         compiler_params=pltpu.CompilerParams(collective_id=0, has_side_effects=True),
         name="block_cg",
-    )(right_sides.reshape(512, 128), spectrum, noise_var.reshape(64, 128), observed.reshape(64, 128), *ws)
+    )(*operands)
     return sol.reshape(8, 16, 4, 128), ng.reshape(16, 4, 128)
 
 

time: 107 us -> 83.7 us (0.78)
  Pallas kernels: 103 us -> 81.7 us
    pallas_call x1, Pallas kernels: 103 us -> 81.7 us  [local(): pl.pallas_call(kernel, out_shape=(pltpu.VMEM((512, 128), F32), pltpu.VMEM...]
    unnamed x4 -> x2, local copies, waits for them, and re-layouts: 2.3 us -> 1.32 us
where the time goes in v2:
time: 83.7 us; the launch traced here: 83.6 us
  Pallas kernels  81.7 us (98%)
  local copies, waits for them, and re-layouts  1.32 us (2%)
    pallas_call x1, Pallas kernels, local(): pl.pallas_call(kernel, out_shape=(pltpu.VMEM((512, 128), F32), pltpu.VMEM...  81.7 us

profile of v2, /device:TPU:1, one launch (start us, length us, event | category | flops | bytes accessed | tf_op | source)
XLA Modules:
  0.0 83.6 jit_solution(15557680050317913214)
XLA Ops:
  0.6 81.7 %block_cg.1 = (f32[512,128]{1,0:T(8,128)S(1)}, f32[64,128]{1,0:T(8,128)S(1)}) custom-call(f32[512,128]{1,0:T(8,128)} %bitcast.7, s32[64,128]{1,0:T(8,128)} %bitcast.8, bf16[256,256]{1,0:T(8,128)(2,1)} %constant.16.clone.refs_2_, f32[64,128]{1,0:T(8,128)} %bitcast.9, f32[4,16,128]{2,1,0:T(8,128)} %refs_4_.1, bf16[512,256]{1,0:T(8,128)(2,1)} %constant.17.clone.refs_5_, ...), custom_call_target="tpu_custom_call" | custom-call | tf_op jit(solution)/shard_map/block_cg/pallas_call | solution.py:440
  82.3 0.7 copy.16
  83.0 0.6 copy.17

commit v3 on v2

--- a/solution.py
+++ b/solution.py
@@ -14,6 +14,10 @@
 BF16 = jnp.bfloat16
 N = 128
 SLAB, PENCIL = 8, 32
+HOPS = (0, 1, 2, 1)
+FAR_FIRST = sorted(
+    [(z, o) for z in range(SLAB) for o in range(16)],
+    key=lambda t: (-(min(t[0], SLAB - t[0]) + HOPS[t[1] & 3] + HOPS[t[1] >> 2]), -min(t[0], SLAB - t[0])))
 INV = 1.0 / (N * N * N)
 
 
@@ -200,22 +204,11 @@
             for c in range(2):
                 to(chip, c, row + core_step * c)
 
-        for offsets in ((4,), (3, 5), (2, 6), (1, 7)):
-            slabs = [(s + so) & 7 for so in offsets]
-            pre = [(ts * 16, base(ts)) for ts in slabs]
-
-            @pl.loop(0, 8)
-            def _(o):
-                for u in range(2):
-                    there = seat ^ (2 * o + u)
-                    step = chip_step * there
-                    for first, row in pre:
-                        to_chip(first + there, row + step)
-
-        @pl.loop(1, 16)
-        def _(o):
+        slabs = [(s + z) & 7 for z in range(SLAB)]
+        pre = [(ts * 16, base(ts)) for ts in slabs]
+        for z, o in FAR_FIRST[:-1]:
             there = seat ^ o
-            to_chip(s * 16 + there, base(s) + chip_step * there)
+            to_chip(pre[z][0] + there, pre[z][1] + chip_step * there)
         to(s * 16 + seat, 1 - core, base(s) + chip_step * seat + core_step * (1 - core))
 
     def wait_rows(ref, n, sem):
@@ -331,7 +324,6 @@
     @pl.loop(1, SLAB)
     def _(o):
         pl.semaphore_signal(enter, inc=1, device_id=((s + o) & 7, p), device_id_type=MESH)
-    pl.semaphore_wait(enter, SLAB - 1)
 
     def lam_rows(owner):
         return lam.at[pl.ds(pl.multiple_of(16 * owner, 16), 16), :]
@@ -342,14 +334,14 @@
             src_ref=spec_ref.at[ts >> 1], dst_ref=lam_rows(s), send_sem=lam_sems.at[0], recv_sem=lam_sems.at[1],
             device_id=(ts, p), device_id_type=MESH).start()
     lam[pl.ds(pl.multiple_of(16 * s, 16), 16), :] = spec_ref[s >> 1]
-
-    forward_send(0, 0)
-    forward_send(0, 1)
+    pl.semaphore_wait(enter, SLAB - 1)
 
     def halves(f):
         @pl.loop(0, 2)
         def _(h):
             f(h)
+
+    halves(lambda h: forward_send(0, h))
 
     def middles(k, between=None):
         def one(h):

time: 83.7 us -> 80.7 us (0.964)
  Pallas kernels: 81.7 us -> 78.7 us
    pallas_call x1, Pallas kernels: 81.7 us -> 78.7 us  [local(): pl.pallas_call(kernel, out_shape=(pltpu.VMEM((512, 128), F32), pltpu.VMEM...]
where the time goes in v3:
time: 80.7 us; the launch traced here: 80.6 us
  Pallas kernels  78.7 us (98%)
  local copies, waits for them, and re-layouts  1.32 us (2%)
    pallas_call x1, Pallas kernels, local(): pl.pallas_call(kernel, out_shape=(pltpu.VMEM((512, 128), F32), pltpu.VMEM...  78.7 us

profile of v3, /device:TPU:1, one launch (start us, length us, event | category | flops | bytes accessed | tf_op | source)
XLA Modules:
  0.0 80.6 jit_solution(5340990468197920674)
XLA Ops:
  0.6 78.7 %block_cg.1 = (f32[512,128]{1,0:T(8,128)S(1)}, f32[64,128]{1,0:T(8,128)S(1)}) custom-call(f32[512,128]{1,0:T(8,128)} %bitcast.7, s32[64,128]{1,0:T(8,128)} %bitcast.8, bf16[256,256]{1,0:T(8,128)(2,1)} %constant.16.clone.refs_2_, f32[64,128]{1,0:T(8,128)} %bitcast.9, f32[4,16,128]{2,1,0:T(8,128)} %refs_4_.1, bf16[512,256]{1,0:T(8,128)(2,1)} %constant.17.clone.refs_5_, ...), custom_call_target="tpu_custom_call" | custom-call | tf_op jit(solution)/shard_map/block_cg/pallas_call | solution.py:432
  79.3 0.7 copy.16
  80.0 0.6 copy.17

commit v4 on v3

--- a/solution.py
+++ b/solution.py
@@ -18,6 +18,7 @@
 FAR_FIRST = sorted(
     [(z, o) for z in range(SLAB) for o in range(16)],
     key=lambda t: (-(min(t[0], SLAB - t[0]) + HOPS[t[1] & 3] + HOPS[t[1] >> 2]), -min(t[0], SLAB - t[0])))
+SEATS = sorted(range(1, PENCIL), key=lambda o: -(HOPS[(o >> 1) & 3] + HOPS[o >> 3]))
 INV = 1.0 / (N * N * N)
 
 
@@ -139,15 +140,14 @@
 
     barrier = pltpu.get_barrier_semaphore()
 
-    @pl.loop(1, PENCIL)
-    def _(o):
+    for load in loads[:4]:
+        load.start()
+    for o in (4, 3, 5, 2, 6, 1, 7):
+        pl.semaphore_signal(barrier, inc=1, device_id=((s + o) & 7, p), device_id_type=MESH)
+    for o in SEATS:
         pl.semaphore_signal(barrier, inc=1, device_id=(s, p ^ o), device_id_type=MESH)
 
-    @pl.loop(1, SLAB)
-    def _(o):
-        pl.semaphore_signal(barrier, inc=1, device_id=((s + o) & 7, p), device_id_type=MESH)
-
-    for load in loads:
+    for load in loads[4:]:
         load.start()
 
     lane = iota((128, 128), 1)
@@ -321,8 +321,7 @@
 
     pl.semaphore_wait(barrier, PENCIL - 1 + SLAB - 1)
 
-    @pl.loop(1, SLAB)
-    def _(o):
+    for o in (4, 3, 5, 2, 6, 1, 7):
         pl.semaphore_signal(enter, inc=1, device_id=((s + o) & 7, p), device_id_type=MESH)
 
     def lam_rows(owner):

time: 80.7 us -> 80.3 us (level)
  no operation moved by 1% of the time
where the time goes in v4:
time: 80.3 us; the launch traced here: 80.2 us
  Pallas kernels  78.3 us (98%)
  local copies, waits for them, and re-layouts  1.32 us (2%)
    pallas_call x1, Pallas kernels, local(): pl.pallas_call(kernel, out_shape=(pltpu.VMEM((512, 128), F32), pltpu.VMEM...  78.3 us

profile of v4, /device:TPU:1, one launch (start us, length us, event | category | flops | bytes accessed | tf_op | source)
XLA Modules:
  0.0 80.2 jit_solution(9873823883863040629)
XLA Ops:
  0.6 78.3 %block_cg.1 = (f32[512,128]{1,0:T(8,128)S(1)}, f32[64,128]{1,0:T(8,128)S(1)}) custom-call(f32[512,128]{1,0:T(8,128)} %bitcast.7, s32[64,128]{1,0:T(8,128)} %bitcast.8, bf16[256,256]{1,0:T(8,128)(2,1)} %constant.16.clone.refs_2_, f32[64,128]{1,0:T(8,128)} %bitcast.9, f32[4,16,128]{2,1,0:T(8,128)} %refs_4_.1, bf16[512,256]{1,0:T(8,128)(2,1)} %constant.17.clone.refs_5_, ...), custom_call_target="tpu_custom_call" | custom-call | tf_op jit(solution)/shard_map/block_cg/pallas_call | solution.py:431
  78.9 0.7 copy.16
  79.6 0.6 copy.17
